TPU v7x, 32 devices: a whole 2x2x4 slice. The times are simulated.
32 devices in a mesh: blk: 8 (over z, y), grp: 4 (over x, core).
Axes of the slice: x: 2, y: 2, z: 4, core: 2. Of those that a mesh axis runs over, the one named last changes fastest.
Arguments:
- embeddings: bfloat16 [4096, 1024], P(('blk', 'grp')), may hold values from -100 to 100
- labels: int32 [4096], P(('blk', 'grp')), may hold values from 0 to 4999, as said below
Outputs:
- anchor_loss: float32 [1024], P(('blk', 'grp'))
- mean_loss: float32 [], replicated
Inputs may be any that keep to these rules, and one draw needn't show every extreme that they name: `labels`: A label of 1000 or more belongs to one sample only.
All inputs are finite; a program needn't handle non-finite values.
Results may differ from a plain program's by a relative error of at most 0.0003.
Values may be sent and summed in bfloat16 or wider, within the bound.
A program may use at most 64 MiB of HBM per device.

v0:
```python
import jax
import jax.numpy as jnp
from jax import lax
from jax.sharding import PartitionSpec as P

A_DEV = 32


def make_fold(anchors, anchor_labels, anchor_ids, key_id_of):

    def fold(carry, pieces, start):
        keys, key_labels = pieces
        where_at = jnp.arange(keys.shape[0], dtype=jnp.int32)
        key_ids = key_id_of(where_at)
        score = (
            lax.dot_general(
                anchors, keys, (((1,), (1,)), ((), ())), preferred_element_type=jnp.float32
            )
            * 10.0
        )
        self_mask = anchor_ids[:, None] == key_ids[None, :]
        expo = jnp.where(self_mask, 0.0, jnp.exp(score - 10.0))
        positive = (anchor_labels[:, None] == key_labels[None, :]) & jnp.logical_not(self_mask)
        return (
            jnp.sum(expo, axis=1),
            jnp.sum(jnp.where(positive, score, 0.0), axis=1),
            jnp.sum(positive.astype(jnp.float32), axis=1),
        )

    return fold


def local(embeddings, labels):
    rows = embeddings.shape[0]
    values = embeddings.astype(jnp.float32)
    unit = (values * lax.rsqrt(jnp.sum(values * values, axis=1, keepdims=True) + 1e-06)).astype(
        jnp.bfloat16
    )
    own_anchors = unit[:A_DEV]
    own_labels = labels[:A_DEV]
    blk_index = lax.axis_index("blk")
    grp_index = lax.axis_index("grp")
    grp_count = lax.axis_size("grp")

    def strided_key(where_at):
        return (where_at // rows * grp_count + grp_index) * rows + where_at % rows

    positions = jnp.arange(A_DEV * grp_count, dtype=jnp.int32)
    anchors, anchor_labels = (
        lax.all_gather(own_anchors, "grp", axis=0, tiled=True),
        lax.all_gather(own_labels, "grp", axis=0, tiled=True),
    )
    anchor_ids = (blk_index * grp_count + positions // A_DEV) * rows + positions % A_DEV
    zeros = jnp.zeros((anchors.shape[0],), jnp.float32)
    fold = make_fold(anchors, anchor_labels, anchor_ids, strided_key)
    totals = fold(
        (zeros, zeros, zeros),
        (
            lax.all_gather(unit, "blk", axis=0, tiled=True),
            lax.all_gather(labels, "blk", axis=0, tiled=True),
        ),
        jnp.int32(0),
    )
    denom, pos_sum, count = (
        lax.psum_scatter(totals[0], "grp", scatter_dimension=0, tiled=True),
        lax.psum_scatter(totals[1], "grp", scatter_dimension=0, tiled=True),
        lax.psum_scatter(totals[2], "grp", scatter_dimension=0, tiled=True),
    )
    valid = count > 0.0
    anchor_loss = jnp.where(valid, jnp.log(denom) + 10.0 - pos_sum / jnp.maximum(count, 1.0), 0.0)
    loss_total, valid_total = lax.psum(
        (jnp.sum(anchor_loss), jnp.sum(valid.astype(jnp.float32))), ("blk", "grp")
    )
    mean_loss = loss_total / jnp.maximum(valid_total, 1.0)
    return (anchor_loss, mean_loss)


def solution(mesh):
    placed = (P(("blk", "grp"), None), P(("blk", "grp")))
    return jax.shard_map(
        local, mesh=mesh, in_specs=placed, out_specs=(P(("blk", "grp")), P()), check_vma=False
    )
```

profile of v0, /device:TPU:0, one launch (start us, length us, event | category | flops | bytes accessed | tf_op | source)
XLA Modules:
  0.0 120.6 jit_solution(12838552396629161836)
XLA Ops:
  7.2 0.0 all-gather.3.cloned.1.call-start
  7.2 1.1 fusion
  8.3 1.8 %fusion.1 = bf16[128,1024]{1,0:T(8,128)(2,1)} fusion(bf16[128,1024]{1,0:T(8,128)(2,1)} %param.2, f32[128]{0:T(128)S(1)} %add_rsqrt_fusion), kind=kLoop, calls=%fused_computation.6 | loop fusion | flops 393216 | bytes 524800 | tf_op jit(solution)/shard_map/convert_element_type | solution.py:36
  10.1 0.0 all-gather.3.cloned.1.call-update
  10.1 0.8 slice.8
  11.0 1.3 %fusion.22 = (u32[1]{0:T(128)}, u32[1]{0:T(128)}) fusion(u32[32]{0:T(128)} %constant.88, u32[]{:T(128)S(6)} %add.107, u32[]{:T(128)S(6)} %add.104), kind=kLoop, calls=%fused_computation.44 | loop fusion | bytes 24
  13.6 0.8 slice_dynamic-update-slice_fusion
  14.4 6.4 %all-reduce = s32[128]{0:T(128)S(1)} all-reduce(s32[128]{0:T(128)S(1)} %slice_dynamic-update-slice_fusion), channel_id=1, replica_groups=mesh['blk'=8,'grp'=4] {'grp'}, use_global_device_ids=true, to_apply=%add | all-reduce | flops 128 | bytes 1024
  20.7 21.0 %all-gather = s32[8,1,128]{2,1,0:T(1,128)S(1)} all-gather(s32[1,1,128]{2,1,0:T(1,128)} %bitcast.7), channel_id=1, replica_groups=mesh['blk'=8,'grp'=4] {'blk'}, dimensions={0}, use_global_device_ids=true | all-gather | bytes 4608 | tf_op jit(solution)/shard_map/all_gather | solution.py:60
  41.7 5.8 %all_gather.14 = bf16[128,1024]{1,0:T(8,128)(2,1)S(1)} all-gather(bf16[32,1024]{1,0:T(8,128)(2,1)S(1)} %slice.8), channel_id=1, replica_groups=mesh['blk'=8,'grp'=4] {'grp'}, dimensions={0}, use_global_device_ids=true | all-gather | bytes 327680 | tf_op jit(solution)/shard_map/all_gather | solution.py:50
  47.5 14.6 %all-gather.3.cloned.1.call-done = bf16[1024,1024]{1,0:T(8,128)(2,1)} async-done(((bf16[128,1024]{1,0:T(8,128)(2,1)}), bf16[1024,1024]{1,0:T(8,128)(2,1)}) %all-gather.3.cloned.1.call-update) | async-done | bytes 2097168 | tf_op jit(solution)/shard_map/all_gather | solution.py:59
  62.1 2.6 %fusion.2 = (f32[128]{0:T(128)S(1)}, f32[128]{0:T(128)S(1)}, f32[128]{0:T(128)S(1)}) fusion(s32[1024]{0:T(1024)S(1)} %fusion.13, s32[128]{0:T(128)S(1)} %fusion.15, s32[1024]{0:T(1024)S(1)} %bitcast.6, s32[128]{0:T(128)S(1)} %all-reduce, bf16[128,1024]{1,0:T(8,128)(2,1)S(1)} %all_gather.14, bf16[1024,1024]{1,0:T(8,128)(2,1)} %all-gather.3.cloned.1.call-done), kind=kOutput, calls=%fused_computation.7 | convolution fusion | flops 270007936 | bytes 2370048 | tf_op jit(solution)/shard_map/dot_general | solution.py:16
  64.8 5.7 %all-reduce.5 = (f32[128]{0:T(128)S(1)}, f32[128]{0:T(128)S(1)}, f32[128]{0:T(128)S(1)}) all-reduce(f32[128]{0:T(128)S(1)} %get-tuple-element.3, f32[128]{0:T(128)S(1)} %get-tuple-element.2, f32[128]{0:T(128)S(1)} %get-tuple-element.4), channel_id=4, replica_groups=mesh['blk'=8,'grp'=4] {'grp'}, use_global_device_ids=true, to_apply=%region_6.7.clone | all-reduce | flops 384 | bytes 3072
  70.4 1.3 %fusion.21 = (f32[]{:T(128)}, f32[32]{0:T(128)}, f32[]{:T(128)}) fusion(f32[128]{0:T(128)S(1)} %get-tuple-element.7, u32[]{:T(128)S(6)} %multiply.4, f32[128]{0:T(128)S(1)} %get-tuple-element.8, f32[128]{0:T(128)S(1)} %get-tuple-element.9), kind=kLoop, calls=%fused_computation.43 | loop fusion | flops 286 | bytes 524 | tf_op jit(solution)/shard_map/reduce_sum | solution.py:72
  71.7 39.7 %all-reduce.4 = (f32[]{:T(128)}, f32[]{:T(128)}) all-reduce(f32[]{:T(128)} %get-tuple-element.10, f32[]{:T(128)} %get-tuple-element.12), channel_id=1, replica_groups=mesh['blk'=8,'grp'=4] {'blk','grp'}, use_global_device_ids=true, to_apply=%region_8.9 | all-reduce | flops 2 | bytes 16 | tf_op jit(solution)/shard_map/psum | solution.py:71
  (4 shorter events, 0.0 us)
Async XLA Ops:
  7.2 54.9 %all-gather.3.cloned.1.call-start = ((), (), s32[]{:S(2)}) async-start(), calls=%async_computation | async-start | bytes 2359296 | tf_op jit(solution)/shard_map/all_gather | solution.py:59
Sparse Core Ops, SparseCore 0:
  10.2 51.8 all-gather.2
where the time goes:
time: 121 us
  blocking collectives  78.5 us (65%)
  between operations  17.7 us (15%)
  waiting for transfers between devices  14.6 us (12%)
  other arithmetic  4.18 us (3%)
  local copies, waits for them, and re-layouts  2.92 us (2%)
  matrix products  2.65 us (2%)
    psum x1, blocking collectives, local(): lax.psum((jnp.sum(anchor_loss), jnp.sum(valid.astype(jnp.float32))), ('bl...  39.7 us
    all_gather x1, blocking collectives, local(): lax.all_gather(labels, 'blk', axis=0, tiled=True)  21 us
    all_gather x1, waiting for transfers between devices, local(): lax.all_gather(unit, 'blk', axis=0, tiled=True)  14.6 us
    unnamed x2, blocking collectives  12 us
    all_gather x1, blocking collectives, local(): lax.all_gather(own_anchors, 'grp', axis=0, tiled=True)  5.76 us
    dot_general x1, matrix products, fold(): lax.dot_general(anchors, keys, (((1,), (1,)), ((), ())), preferred_elemen...  2.65 us
  transfers between devices with their start and end apart: 1, of which 1 were waited for; matrix products, arithmetic and copies ran while one was open for 2% of the time, Pallas kernels for 0%

commit v1 on v0

--- a/solution.py
+++ b/solution.py
@@ -69,7 +69,7 @@
     valid = count > 0.0
     anchor_loss = jnp.where(valid, jnp.log(denom) + 10.0 - pos_sum / jnp.maximum(count, 1.0), 0.0)
     loss_total, valid_total = lax.psum(
-        (jnp.sum(anchor_loss), jnp.sum(valid.astype(jnp.float32))), ("blk", "grp")
+        lax.psum((jnp.sum(anchor_loss), jnp.sum(valid.astype(jnp.float32))), "grp"), "blk"
     )
     mean_loss = loss_total / jnp.maximum(valid_total, 1.0)
     return (anchor_loss, mean_loss)

time: 121 us -> 108 us (0.89)
  blocking collectives: 78.5 us -> 65.7 us
    psum x1 -> x2, blocking collectives: 39.7 us -> 26.9 us  [the longest x1 19.6 us: local(): lax.psum(lax.psum((jnp.sum(anchor_loss), jnp.sum(valid.astype(jnp.float32...]
  transfers between devices with their start and end apart: 1 -> 1, of which waited for: 1 -> 1; matrix products, arithmetic and copies ran while one was open for 2% -> 3% of each run, Pallas kernels for 0% -> 0%
where the time goes in v1:
time: 108 us
  blocking collectives  65.7 us (61%)
  between operations  17.7 us (16%)
  waiting for transfers between devices  14.6 us (14%)
  other arithmetic  4.09 us (4%)
  local copies, waits for them, and re-layouts  2.92 us (3%)
  matrix products  2.65 us (2%)
    all_gather x1, blocking collectives, local(): lax.all_gather(labels, 'blk', axis=0, tiled=True)  21 us
    psum x1, blocking collectives, local(): lax.psum(lax.psum((jnp.sum(anchor_loss), jnp.sum(valid.astype(jnp.float32...  19.6 us
    all_gather x1, waiting for transfers between devices, local(): lax.all_gather(unit, 'blk', axis=0, tiled=True)  14.6 us
    unnamed x2, blocking collectives  12 us
    psum x1, blocking collectives, local(): lax.psum((jnp.sum(anchor_loss), jnp.sum(valid.astype(jnp.float32))), 'grp')  7.28 us
    all_gather x1, blocking collectives, local(): lax.all_gather(own_anchors, 'grp', axis=0, tiled=True)  5.76 us
    dot_general x1, matrix products, fold(): lax.dot_general(anchors, keys, (((1,), (1,)), ((), ())), preferred_elemen...  2.65 us
  transfers between devices with their start and end apart: 1, of which 1 were waited for; matrix products, arithmetic and copies ran while one was open for 3% of the time, Pallas kernels for 0%

profile of v1, /device:TPU:0, one launch (start us, length us, event | category | flops | bytes accessed | tf_op | source)
XLA Modules:
  0.0 107.7 jit_solution(8831264422006213549)
XLA Ops:
  7.2 0.0 all-gather.3.cloned.1.call-start
  7.2 1.1 %fusion = f32[128]{0:T(128)S(1)} fusion(bf16[128,1024]{1,0:T(8,128)(2,1)} %param.2), kind=kLoop, calls=%fused_computation.5 | loop fusion | flops 393088 | bytes 262656 | tf_op jit(solution)/shard_map/reduce_sum | solution.py:36
  8.3 1.8 %fusion.1 = bf16[128,1024]{1,0:T(8,128)(2,1)} fusion(bf16[128,1024]{1,0:T(8,128)(2,1)} %param.2, f32[128]{0:T(128)S(1)} %add_rsqrt_fusion), kind=kLoop, calls=%fused_computation.6 | loop fusion | flops 393216 | bytes 524800 | tf_op jit(solution)/shard_map/convert_element_type | solution.py:36
  10.1 0.0 all-gather.3.cloned.1.call-update
  10.1 0.8 slice.8
  11.0 1.3 %fusion.22 = (u32[1]{0:T(128)}, u32[1]{0:T(128)}) fusion(u32[32]{0:T(128)} %constant.88, u32[]{:T(128)S(6)} %add.111, u32[]{:T(128)S(6)} %add.108), kind=kLoop, calls=%fused_computation.44 | loop fusion | bytes 24
  13.6 0.8 slice_dynamic-update-slice_fusion
  14.4 6.4 %all-reduce = s32[128]{0:T(128)S(1)} all-reduce(s32[128]{0:T(128)S(1)} %slice_dynamic-update-slice_fusion), channel_id=1, replica_groups=mesh['blk'=8,'grp'=4] {'grp'}, use_global_device_ids=true, to_apply=%add | all-reduce | flops 128 | bytes 1024
  20.7 21.0 %all-gather = s32[8,1,128]{2,1,0:T(1,128)S(1)} all-gather(s32[1,1,128]{2,1,0:T(1,128)} %bitcast.7), channel_id=1, replica_groups=mesh['blk'=8,'grp'=4] {'blk'}, dimensions={0}, use_global_device_ids=true | all-gather | bytes 4608 | tf_op jit(solution)/shard_map/all_gather | solution.py:60
  41.7 5.8 %all_gather.14 = bf16[128,1024]{1,0:T(8,128)(2,1)S(1)} all-gather(bf16[32,1024]{1,0:T(8,128)(2,1)S(1)} %slice.8), channel_id=1, replica_groups=mesh['blk'=8,'grp'=4] {'grp'}, dimensions={0}, use_global_device_ids=true | all-gather | bytes 327680 | tf_op jit(solution)/shard_map/all_gather | solution.py:50
  47.5 14.6 %all-gather.3.cloned.1.call-done = bf16[1024,1024]{1,0:T(8,128)(2,1)} async-done(((bf16[128,1024]{1,0:T(8,128)(2,1)}), bf16[1024,1024]{1,0:T(8,128)(2,1)}) %all-gather.3.cloned.1.call-update) | async-done | bytes 2097168 | tf_op jit(solution)/shard_map/all_gather | solution.py:59
  62.1 2.6 %fusion.2 = (f32[128]{0:T(128)S(1)}, f32[128]{0:T(128)S(1)}, f32[128]{0:T(128)S(1)}) fusion(s32[1024]{0:T(1024)S(1)} %fusion.13, s32[128]{0:T(128)S(1)} %fusion.15, s32[1024]{0:T(1024)S(1)} %bitcast.6, s32[128]{0:T(128)S(1)} %all-reduce, bf16[128,1024]{1,0:T(8,128)(2,1)S(1)} %all_gather.14, bf16[1024,1024]{1,0:T(8,128)(2,1)} %all-gather.3.cloned.1.call-done), kind=kOutput, calls=%fused_computation.7 | convolution fusion | flops 270007936 | bytes 2370048 | tf_op jit(solution)/shard_map/dot_general | solution.py:16
  64.8 5.7 %all-reduce.6 = (f32[128]{0:T(128)S(1)}, f32[128]{0:T(128)S(1)}, f32[128]{0:T(128)S(1)}) all-reduce(f32[128]{0:T(128)S(1)} %get-tuple-element.3, f32[128]{0:T(128)S(1)} %get-tuple-element.2, f32[128]{0:T(128)S(1)} %get-tuple-element.4), channel_id=4, replica_groups=mesh['blk'=8,'grp'=4] {'grp'}, use_global_device_ids=true, to_apply=%region_6.7.clone | all-reduce | flops 384 | bytes 3072
  70.4 1.2 %fusion.21 = (f32[]{:T(128)}, f32[32]{0:T(128)}, f32[]{:T(128)}) fusion(f32[128]{0:T(128)S(1)} %get-tuple-element.9, u32[]{:T(128)S(6)} %multiply.4, f32[128]{0:T(128)S(1)} %get-tuple-element.10, f32[128]{0:T(128)S(1)} %get-tuple-element.11), kind=kLoop, calls=%fused_computation.43 | loop fusion | flops 286 | bytes 524 | tf_op jit(solution)/shard_map/reduce_sum | solution.py:72
  71.6 7.3 %all-reduce.5 = (f32[]{:T(128)}, f32[]{:T(128)}) all-reduce(f32[]{:T(128)} %get-tuple-element.12, f32[]{:T(128)} %get-tuple-element.14), channel_id=1, replica_groups=mesh['blk'=8,'grp'=4] {'grp'}, use_global_device_ids=true, to_apply=%region_8.9 | all-reduce | flops 2 | bytes 16 | tf_op jit(solution)/shard_map/psum | solution.py:72
  78.9 19.6 %all-reduce.4 = (f32[]{:T(128)}, f32[]{:T(128)}) all-reduce(f32[]{:T(128)} %get-tuple-element.7, f32[]{:T(128)} %get-tuple-element.8), channel_id=1, replica_groups=mesh['blk'=8,'grp'=4] {'blk'}, use_global_device_ids=true, to_apply=%region_9.10 | all-reduce | flops 2 | bytes 16 | tf_op jit(solution)/shard_map/psum | solution.py:71
  (4 shorter events, 0.0 us)
Async XLA Ops:
  7.2 54.9 %all-gather.3.cloned.1.call-start = ((), (), s32[]{:S(2)}) async-start(), calls=%async_computation | async-start | bytes 2359296 | tf_op jit(solution)/shard_map/all_gather | solution.py:59
Sparse Core Ops, SparseCore 0:
  10.2 51.8 all-gather.2

commit v2 on v0

--- a/solution.py
+++ b/solution.py
@@ -56,7 +56,9 @@
     totals = fold(
         (zeros, zeros, zeros),
         (
-            lax.all_gather(unit, "blk", axis=0, tiled=True),
+            jnp.concatenate(
+                lax.all_to_all(jnp.stack([unit] * lax.axis_size("blk")), "blk", 0, 0), axis=0
+            ),
             lax.all_gather(labels, "blk", axis=0, tiled=True),
         ),
         jnp.int32(0),

time: 121 us -> 126 us (1.041)
  blocking collectives: 78.5 us -> 107 us
  waiting for transfers between devices: 14.6 us -> 0.01 us
  between operations: 17.7 us -> 4.33 us
  starting transfers between devices: 0.04 us -> 7.44 us
  matrix products: 2.65 us -> 1.06 us
    all_gather x1, blocking collectives: 21 us -> 42.6 us  [local(): lax.all_gather(labels, 'blk', axis=0, tiled=True)]
    all_gather x1 -> x0, waiting for transfers between devices: 14.6 us -> none  [local(): lax.all_gather(unit, 'blk', axis=0, tiled=True)]
    all_to_all x0 -> x1, starting transfers between devices: none -> 7.44 us  [local(): lax.all_to_all(jnp.stack([unit] * lax.axis_size('blk')), 'blk', 0, 0)]
    psum x1, blocking collectives: 39.7 us -> 46.3 us  [local(): lax.psum((jnp.sum(anchor_loss), jnp.sum(valid.astype(jnp.float32))), ('bl...]
    another operation x0 -> x1, local copies, waits for them, and re-layouts: none -> 1.62 us  [local(): jnp.stack([unit] * lax.axis_size('blk'))]
    dot_general x1, matrix products: 2.65 us -> 1.06 us  [fold(): lax.dot_general(anchors, keys, (((1,), (1,)), ((), ())), preferred_elemen...]
    unnamed x3 -> x7, local copies, waits for them, and re-layouts: 2.07 us -> 0.7 us
  transfers between devices with their start and end apart: 1 -> 1, of which waited for: 1 -> 0; matrix products, arithmetic and copies ran while one was open for 2% -> 1% of each run, Pallas kernels for 0% -> 0%
where the time goes in v2:
time: 126 us; the launch traced here: 125 us
  blocking collectives  107 us (85%)
  starting transfers between devices  7.44 us (6%)
  between operations  4.33 us (3%)
  other arithmetic  3.45 us (3%)
  local copies, waits for them, and re-layouts  2.32 us (2%)
    psum x1, blocking collectives, local(): lax.psum((jnp.sum(anchor_loss), jnp.sum(valid.astype(jnp.float32))), ('bl...  46.3 us
    all_gather x1, blocking collectives, local(): lax.all_gather(labels, 'blk', axis=0, tiled=True)  42.6 us
    unnamed x2, blocking collectives  12 us
    all_to_all x1, starting transfers between devices, local(): lax.all_to_all(jnp.stack([unit] * lax.axis_size('blk')), 'blk', 0, 0)  7.44 us
    all_gather x1, blocking collectives, local(): lax.all_gather(own_anchors, 'grp', axis=0, tiled=True)  5.76 us
  transfers between devices with their start and end apart: 1, of which 0 were waited for; matrix products, arithmetic and copies ran while one was open for 1% of the time, Pallas kernels for 0%

profile of v2, /device:TPU:0, one launch (start us, length us, event | category | flops | bytes accessed | tf_op | source)
XLA Modules:
  0.0 125.3 jit_solution(2691134075254960675)
XLA Ops:
  0.6 1.1 fusion
  1.7 1.1 fusion.1
  2.8 1.6 %stack.2 = bf16[8,128,1024]{2,1,0:T(8,128)(2,1)} broadcast(bf16[128,1024]{1,0:T(8,128)(2,1)S(1)} %fusion.1), dimensions={1,2} | broadcast | bytes 2359296 | tf_op jit(solution)/shard_map/stack | solution.py:60
  4.4 0.0 copy-start
  4.4 0.0 copy-start.1
  4.4 7.4 %all-to-all-start = ((bf16[8,128,1024]{2,1,0:T(8,128)(2,1)}), bf16[8,128,1024]{2,1,0:T(8,128)(2,1)S(1)}, u32[]{:S(2)}, u32[]{:S(2)}) async-start(bf16[8,128,1024]{2,1,0:T(8,128)(2,1)} %stack.2), calls=%async_computation | async-start | bytes 4194304 | tf_op jit(solution)/shard_map/all_to_all | solution.py:60
  11.9 0.0 copy-done
  11.9 0.6 fusion.22
  13.8 0.0 copy-done.1
  13.8 0.1 slice_dynamic-update-slice_fusion
  13.9 4.9 %all-reduce = s32[128]{0:T(128)S(1)} all-reduce(s32[128]{0:T(128)S(1)} %slice_dynamic-update-slice_fusion), channel_id=1, replica_groups=mesh['blk'=8,'grp'=4] {'grp'}, use_global_device_ids=true, to_apply=%add | all-reduce | flops 128 | bytes 1024
  18.8 42.6 %all-gather = s32[8,1,128]{2,1,0:T(1,128)S(1)} all-gather(s32[1,1,128]{2,1,0:T(1,128)S(1)} %bitcast.9), channel_id=1, replica_groups=mesh['blk'=8,'grp'=4] {'blk'}, dimensions={0}, use_global_device_ids=true | all-gather | bytes 4608 | tf_op jit(solution)/shard_map/all_gather | solution.py:62
  61.5 5.8 %all_gather.11 = bf16[128,1024]{1,0:T(8,128)(2,1)S(1)} all-gather(bf16[32,1024]{1,0:T(8,128)(2,1)S(1)} %slice.8), channel_id=1, replica_groups=mesh['blk'=8,'grp'=4] {'grp'}, dimensions={0}, use_global_device_ids=true | all-gather | bytes 327680 | tf_op jit(solution)/shard_map/all_gather | solution.py:50
  67.2 0.0 all-to-all-done
  67.2 1.1 fusion.2
  68.3 7.1 %all-reduce.5 = (f32[128]{0:T(128)S(1)}, f32[128]{0:T(128)S(1)}, f32[128]{0:T(128)S(1)}) all-reduce(f32[128]{0:T(128)S(1)} %get-tuple-element.3, f32[128]{0:T(128)S(1)} %get-tuple-element.2, f32[128]{0:T(128)S(1)} %get-tuple-element.4), channel_id=4, replica_groups=mesh['blk'=8,'grp'=4] {'grp'}, use_global_device_ids=true, to_apply=%region_6.7.clone | all-reduce | flops 384 | bytes 3072
  75.4 1.3 %fusion.21 = (f32[]{:T(128)}, f32[32]{0:T(128)}, f32[]{:T(128)}) fusion(f32[128]{0:T(128)S(1)} %get-tuple-element.7, u32[]{:T(128)S(6)} %multiply.4, f32[128]{0:T(128)S(1)} %get-tuple-element.8, f32[128]{0:T(128)S(1)} %get-tuple-element.9), kind=kLoop, calls=%fused_computation.43 | loop fusion | flops 286 | bytes 524 | tf_op jit(solution)/shard_map/reduce_sum | solution.py:74
  76.7 46.3 %all-reduce.4 = (f32[]{:T(128)}, f32[]{:T(128)}) all-reduce(f32[]{:T(128)} %get-tuple-element.10, f32[]{:T(128)} %get-tuple-element.12), channel_id=1, replica_groups=mesh['blk'=8,'grp'=4] {'blk','grp'}, use_global_device_ids=true, to_apply=%region_8.9 | all-reduce | flops 2 | bytes 16 | tf_op jit(solution)/shard_map/psum | solution.py:73
  (5 shorter events, 0.0 us)
Async XLA Ops:
  4.4 7.5 %copy-start = (u32[32]{0:T(128)S(1)}, u32[32]{0:T(128)}, u32[]{:S(2)}) copy-start(u32[32]{0:T(128)} %constant.88) | copy-start | bytes 388
  4.4 9.4 %copy-start.1 = (s32[128]{0:T(128)S(1)}, s32[128]{0:T(128)}, u32[]{:S(2)}) copy-start(s32[128]{0:T(128)} %param.3) | copy-start | bytes 1540
  4.4 62.8 %all-to-all-start = ((bf16[8,128,1024]{2,1,0:T(8,128)(2,1)}), bf16[8,128,1024]{2,1,0:T(8,128)(2,1)S(1)}, u32[]{:S(2)}, u32[]{:S(2)}) async-start(bf16[8,128,1024]{2,1,0:T(8,128)(2,1)} %stack.2), calls=%async_computation | async-start | bytes 4194304 | tf_op jit(solution)/shard_map/all_to_all | solution.py:60
